TPU v7x, 512 devices: a whole 4x8x8 slice. The times are simulated.
512 devices in a mesh: dp: 8 (over x, core), expert: 64 (over z, y).
Axes of the slice: x: 4, y: 8, z: 8, core: 2. Of those that a mesh axis runs over, the one named last changes fastest.
Arguments:
- tokens: bfloat16 [65536, 2048], P(('dp', 'expert')), may hold values from -160 to 160
- router_weight: bfloat16 [2048, 64], replicated, may hold values from -0.25 to 0.25
- route_ids: int32 [65536, 2], P(('dp', 'expert')), may hold values from 0 to 63, as said below
- gate_weight: bfloat16 [64, 768, 2048], P('expert', 'dp'), may hold values from -0.125 to 0.125
- up_weight: bfloat16 [64, 768, 2048], P('expert', 'dp'), may hold values from -0.125 to 0.125
- down_weight: bfloat16 [64, 768, 2048], P('expert', 'dp'), may hold values from -0.21875 to 0.21875
Outputs:
- mixture: bfloat16 [65536, 2048], P(('dp', 'expert'))
- z_loss: float32 [], replicated
Inputs may be any that keep to these rules, and one draw needn't show every extreme that they name: `route_ids`: each row names 2 different experts; among the rows of one device no expert is named more than 5 times, and one expert is named exactly 5 times by the rows of every device.
All inputs are finite; a program needn't handle non-finite values.
Results may differ from a plain program's by a relative error of at most 0.0057.
Values may be sent and summed in bfloat16 or wider, within the bound.
A program may use at most 64 MiB of HBM per device.

v0:
```python
import jax
import jax.numpy as jnp
from jax import lax
from jax.sharding import Mesh
from jax.sharding import PartitionSpec as P

EXPERT = ("expert_0", "expert_1")
DP = ("dp_0", "dp_1")
DP_EXPERT = ("dp_0", "dp_1", "expert_0", "expert_1")


def side_by_side(arrays, axis, dim, along):
    widths = [a.shape[along] for a in arrays]
    both = jnp.concatenate(arrays, axis=along)
    result = lax.all_gather(both, axis, axis=dim, tiled=True)
    return tuple(jnp.split(result, [sum(widths[:k]) for k in range(1, len(widths))], axis=along))


def over_axes(x, axes):
    for axis in axes:
        x = lax.psum(x, axis)
    return x


def slot_index(route_ids, experts, capacity):
    flat_ids = route_ids.reshape(-1)
    onehot = (flat_ids[:, None] == jnp.arange(experts, dtype=jnp.int32)[None, :]).astype(jnp.int32)
    before = jnp.cumsum(onehot, axis=0) - onehot
    position = jnp.sum(before * onehot, axis=1)
    return flat_ids * capacity + position


def on_device(tokens, router_weight, route_ids, gate_weight, up_weight, down_weight):
    rows_here, model_width = tokens.shape
    top_count = route_ids.shape[1]
    experts = router_weight.shape[1]
    owners = lax.axis_size(EXPERT)
    local_experts = gate_weight.shape[0]
    capacity = 5 * rows_here * top_count // (4 * experts)
    logits = jnp.dot(tokens, router_weight, preferred_element_type=jnp.float32)
    log_total = jax.nn.logsumexp(logits, axis=1)
    local_sum = jnp.sum(log_total * log_total)
    chosen = jnp.take_along_axis(logits, route_ids, axis=1)
    route_weight = jax.nn.softmax(chosen, axis=1)
    slots = slot_index(route_ids, experts, capacity)
    pair_count = slots.shape[0]
    slot_match = slots[None, :] == jnp.arange(experts * capacity, dtype=jnp.int32)[:, None]
    token_of = jnp.arange(pair_count, dtype=jnp.int32) // top_count
    source_row = jnp.sum(jnp.where(slot_match, token_of[None, :], 0), axis=1)
    filled = jnp.any(slot_match, axis=1)
    dispatch = jnp.where(filled[:, None], tokens[source_row], jnp.zeros((), tokens.dtype))
    dispatch = dispatch.reshape(experts, capacity, model_width)
    gate_full, up_full, down_full = side_by_side((gate_weight, up_weight, down_weight), DP, 1, 0)
    arrived = lax.all_to_all(dispatch, EXPERT, split_axis=0, concat_axis=0, tiled=True)
    count = arrived.shape[1]
    rows = arrived.reshape(owners, local_experts, count, model_width)
    rows = rows.transpose(1, 0, 2, 3).reshape(local_experts, owners * count, model_width)
    gate_val = jnp.einsum("erd,efd->erf", rows, gate_full, preferred_element_type=jnp.float32)
    up_val = jnp.einsum("erd,efd->erf", rows, up_full, preferred_element_type=jnp.float32)
    hidden = (jax.nn.silu(gate_val) * up_val).astype(jnp.bfloat16)
    result = jnp.einsum(
        "erf,efd->erd", hidden, down_full, preferred_element_type=jnp.float32
    ).astype(jnp.bfloat16)
    result = result.reshape(local_experts, owners, count, model_width)
    result = result.transpose(1, 0, 2, 3).reshape(experts, count, model_width)
    returned = lax.all_to_all(result, EXPERT, split_axis=0, concat_axis=0, tiled=True)
    flat_rows = returned.reshape(experts * capacity, model_width)
    picked = flat_rows[slots].reshape(rows_here, top_count, model_width)
    mixed_out = jnp.sum(route_weight[:, :, None] * picked.astype(jnp.float32), axis=1).astype(
        jnp.bfloat16
    )
    total_sum = over_axes(local_sum, DP_EXPERT)
    token_total = rows_here * lax.axis_size(DP) * owners
    z_loss = total_sum / jnp.float32(token_total)
    return (mixed_out, z_loss)


def solution(mesh):
    split = Mesh(mesh.devices.reshape(4, 2, 8, 8), ("dp_0", "dp_1", "expert_0", "expert_1"))
    return jax.shard_map(
        on_device,
        mesh=split,
        in_specs=(
            P(DP_EXPERT, None),
            P(),
            P(DP_EXPERT, None),
            P(EXPERT, DP, None),
            P(EXPERT, DP, None),
            P(EXPERT, DP, None),
        ),
        out_specs=(P(DP_EXPERT, None), P()),
        check_vma=False,
    )
```

profile of v0, /device:TPU:2, one launch (start us, length us, event | category | flops | bytes accessed | tf_op | source)
XLA Modules:
  0.0 207.8 jit_solution(12558273367088243226)
XLA Ops:
  7.2 2.4 %pad_maximum_fusion = bf16[3,96,2048]{2,1,0:T(8,128)(2,1)} fusion(bf16[1,96,2048]{2,1,0:T(8,128)(2,1)} %param.11, bf16[1,96,2048]{2,1,0:T(8,128)(2,1)} %param.10, bf16[1,96,2048]{2,1,0:T(8,128)(2,1)} %param.9), kind=kLoop, calls=%fused_computation.14 | loop fusion | flops 1179648 | bytes 2359296 | tf_op jit(solution)/shard_map/concatenate | solution.py:14
  9.8 0.1 eq.39
  10.0 0.1 reshape.163
  10.1 0.6 reduce-window.6
  10.7 0.2 slice_reduce_fusion
  11.1 0.1 select_reduce_fusion
  11.3 3.0 %gather_fusion = bf16[320,2048]{1,0:T(8,128)(2,1)} fusion(bf16[128,2048]{1,0:T(8,128)(2,1)S(1)} %copy-done, s32[1024]{0:T(1024)S(1)} %pad_clamp_fusion.1), kind=kCustom, calls=%fused_computation | custom fusion | bytes 2622720 | tf_op jit(solution)/shard_map/gather | solution.py:51
  14.3 2.4 %gather.14 = bf16[64,5,2048]{2,1,0:T(8,128)(2,1)S(1)} reshape(bf16[320,2048]{1,0:T(8,128)(2,1)} %gather_fusion) | data formatting | bytes 2621440 | tf_op jit(solution)/shard_map/gather | solution.py:51
  16.7 0.1 fusion.12
  16.8 0.2 broadcast_in_dim.45
  17.0 0.3 broadcast_select_fusion
  17.3 68.6 %all_to_all.10 = bf16[64,5,2048]{2,1,0:T(8,128)(2,1)S(1)} all-to-all(bf16[64,5,2048]{2,1,0:T(8,128)(2,1)S(1)} %broadcast_select_fusion), channel_id=1, replica_groups=mesh['dp_0'=4,'dp_1'=2,'expert_0'=8,'expert_1'=8] {'expert_0','expert_1'}, dimensions={0} | all-to-all | bytes 2621440 | tf_op jit(solution)/shard_map/all_to_all | solution.py:54
  85.8 1.4 reshape.165
  87.3 4.6 %fusion.2 = f32[320,768]{1,0:T(8,128)} fusion(bf16[320,2048]{1,0:T(8,128)(2,1)} %reshape.165, bf16[3,768,2048]{2,1,0:T(8,128)(2,1)} %all-gather.2.cloned.1.call-done), kind=kOutput, calls=%fused_computation.8 | convolution fusion | flops 1006632960 | bytes 5439488 | tf_op jit(solution)/shard_map/erd,efd->erf/dot_general | solution.py:58
  91.8 5.8 %fusion.3 = bf16[320,2048]{1,0:T(8,128)(2,1)S(1)} fusion(bf16[3,768,2048]{2,1,0:T(8,128)(2,1)} %all-gather.2.cloned.1.call-done, bf16[320,2048]{1,0:T(8,128)(2,1)S(1)} %copy-done.1, f32[320,768]{1,0:T(8,128)} %fusion.2), kind=kOutput, calls=%fused_computation.9 | convolution fusion | flops 2015395840 | bytes 9895936 | tf_op jit(solution)/shard_map/erf,efd->erd/dot_general | solution.py:61
  97.6 1.6 reshape_transpose_reshape.4
  99.2 9.4 %all-to-all-start.1 = ((bf16[64,5,2048]{2,1,0:T(8,128)(2,1)}), bf16[64,5,2048]{2,1,0:T(8,128)(2,1)}, u32[]{:S(2)}, u32[]{:S(2)}) async-start(bf16[64,5,2048]{2,1,0:T(8,128)(2,1)} %reshape_transpose_reshape.4), calls=%async_computation.1 | async-start | bytes 4194304 | tf_op jit(solution)/shard_map/all_to_all | solution.py:66
  108.6 0.3 fusion.22
  109.0 0.6 multiply_reduce_fusion.1
  109.6 9.2 %psum.28 = f32[]{:T(128)} all-reduce(f32[]{:T(128)} %multiply_reduce_fusion.1), channel_id=1, replica_groups=mesh['dp_0'=4,'dp_1'=2,'expert_0'=8,'expert_1'=8] {'dp_0'}, use_global_device_ids=true, to_apply=%region_11.12 | all-reduce | flops 1 | bytes 8 | tf_op jit(solution)/shard_map/psum | solution.py:21
  118.8 3.1 %psum.29 = f32[]{:T(128)} all-reduce(f32[]{:T(128)} %psum.28), channel_id=1, replica_groups=mesh['dp_0'=4,'dp_1'=2,'expert_0'=8,'expert_1'=8] {'dp_1'}, use_global_device_ids=true, to_apply=%region_12.13 | all-reduce | flops 1 | bytes 8 | tf_op jit(solution)/shard_map/psum | solution.py:21
  121.9 38.9 %psum.30 = f32[]{:T(128)} all-reduce(f32[]{:T(128)} %psum.29), channel_id=1, replica_groups=mesh['dp_0'=4,'dp_1'=2,'expert_0'=8,'expert_1'=8] {'expert_0'}, use_global_device_ids=true, to_apply=%region_13.14 | all-reduce | flops 1 | bytes 8 | tf_op jit(solution)/shard_map/psum | solution.py:21
  160.8 24.1 %psum.31 = f32[]{:T(128)} all-reduce(f32[]{:T(128)} %psum.30), channel_id=1, replica_groups=mesh['dp_0'=4,'dp_1'=2,'expert_0'=8,'expert_1'=8] {'expert_1'}, use_global_device_ids=true, to_apply=%region_14.15 | all-reduce | flops 1 | bytes 8 | tf_op jit(solution)/shard_map/psum | solution.py:21
  184.9 0.1 copy.33
  185.1 0.1 mul.55
  185.3 0.1 reshape.187
  185.5 2.0 gather_fusion.2
  187.4 0.1 reshape.190
  188.5 2.6 %reshape.169 = bf16[320,2048]{1,0:T(8,128)(2,1)S(1)} reshape(bf16[64,5,2048]{2,1,0:T(8,128)(2,1)} %all-to-all-done.1) | data formatting | bytes 2621440 | tf_op jit(solution)/shard_map/reshape | solution.py:67
  191.1 2.3 %gather_fusion.1 = bf16[256,2048]{1,0:T(8,128)(2,1)} fusion(bf16[320,2048]{1,0:T(8,128)(2,1)S(1)} %reshape.169, s32[1024]{0:T(1024)S(1)} %pad_clamp_fusion), kind=kCustom, calls=%fused_computation.1 | custom fusion | bytes 2098176 | tf_op jit(solution)/shard_map/gather | solution.py:68
  193.5 2.4 %reshape.170 = f32[128,2,2048]{2,1,0:T(2,128)S(1)} reshape(bf16[256,2048]{1,0:T(8,128)(2,1)} %gather_fusion.1) | data formatting | bytes 3145728 | tf_op jit(solution)/shard_map/convert_element_type | solution.py:69
  195.8 4.0 %multiply_reduce_fusion = bf16[128,2048]{1,0:T(8,128)(2,1)} fusion(f32[128,2,2048]{2,1,0:T(2,128)S(1)} %reshape.170, f32[128,2]{1,0:T(8,128)S(1)} %copy.29), kind=kLoop, calls=%fused_computation.10 | loop fusion | flops 786432 | bytes 2622464 | tf_op jit(solution)/shard_map/reduce_sum | solution.py:69
  (32 shorter events, 0.8 us)
Async XLA Ops:
  7.2 4.1 %copy-start = (bf16[128,2048]{1,0:T(8,128)(2,1)S(1)}, bf16[128,2048]{1,0:T(8,128)(2,1)}, u32[]{:S(2)}) copy-start(bf16[128,2048]{1,0:T(8,128)(2,1)} %param.6) | copy-start | bytes 1572868
  7.2 2.5 %copy-start.3 = (s32[128,2]{0,1:T(2,128)S(1)}, s32[128,2]{0,1:T(2,128)}, u32[]{:S(2)}) copy-start(s32[128,2]{0,1:T(2,128)} %param.8) | copy-start | bytes 3076
  7.2 80.1 %all-gather.2.cloned.1.call-start = ((), (), s32[]{:S(2)}) async-start(), calls=%async_computation.2 | async-start | bytes 10616832 | tf_op jit(solution)/shard_map/all_gather | solution.py:15
  87.2 4.6 %copy-start.1 = (bf16[320,2048]{1,0:T(8,128)(2,1)S(1)}, bf16[320,2048]{1,0:T(8,128)(2,1)}, u32[]{:S(2)}) copy-start(bf16[320,2048]{1,0:T(8,128)(2,1)} %reshape.165) | copy-start | bytes 3932164
  99.2 9.4 %copy-start.2 = (bf16[2048,64]{0,1:T(8,128)(2,1)S(1)}, bf16[2048,64]{0,1:T(8,128)(2,1)}, u32[]{:S(2)}) copy-start(bf16[2048,64]{0,1:T(8,128)(2,1)} %param.7) | copy-start | bytes 786436
  99.2 89.3 %all-to-all-start.1 = ((bf16[64,5,2048]{2,1,0:T(8,128)(2,1)}), bf16[64,5,2048]{2,1,0:T(8,128)(2,1)}, u32[]{:S(2)}, u32[]{:S(2)}) async-start(bf16[64,5,2048]{2,1,0:T(8,128)(2,1)} %reshape_transpose_reshape.4), calls=%async_computation.1 | async-start | bytes 4194304 | tf_op jit(solution)/shard_map/all_to_all | solution.py:66
Sparse Core Ops, SparseCore 0:
  10.1 63.3 all-gather.1
where the time goes:
time: 208 us
  blocking collectives  144 us (69%)
  local copies, waits for them, and re-layouts  19.2 us (9%)
  between operations  16 us (8%)
  matrix products  10.7 us (5%)
  starting transfers between devices  9.44 us (5%)
  other arithmetic  8.59 us (4%)
    psum x4, blocking collectives, over_axes(): x = lax.psum(x, axis)  75.4 us
    all_to_all x1, blocking collectives, on_device(): lax.all_to_all(dispatch, EXPERT, split_axis=0, concat_axis=0, tiled=True)  68.6 us
    all_to_all x1, starting transfers between devices, on_device(): lax.all_to_all(result, EXPERT, split_axis=0, concat_axis=0, tiled=True)  9.41 us
    dot_general x1, matrix products, on_device(): jnp.einsum('erf,efd->erd', hidden, down_full, preferred_element_type=jnp....  5.78 us
    gather x2, local copies, waits for them, and re-layouts, on_device(): tokens[source_row]  5.4 us
    dot_general x1, matrix products, on_device(): jnp.einsum('erd,efd->erf', rows, gate_full, preferred_element_type=jnp.fl...  4.57 us
  transfers between devices with their start and end apart: 2, of which 0 were waited for; matrix products, arithmetic and copies ran while one was open for 6% of the time, Pallas kernels for 0%

commit v1 on v0

v1 whole, which is shorter than its diff:
```python
import functools

import jax
import jax.numpy as jnp
from jax import lax
from jax.experimental import pallas as pl
from jax.experimental.pallas import tpu as pltpu
from jax.sharding import PartitionSpec as P

MESH = pl.DeviceIdType.MESH
BOTH = ("dp", "expert")
RING = 8
CAPACITY = 5
SEGS = 16
LANES = 128
BLOCK = CAPACITY * SEGS
SLOTS = RING * RING * CAPACITY
NT = (((1,), (1,)), ((), ()))
TN = (((0,), (0,)), ((), ()))
NN = (((1,), (0,)), ((), ()))
OFFSETS = (1, 7, 2, 6, 3, 5, 4)


def dot(a, b, dims):
    return lax.dot_general(a, b, dims, preferred_element_type=jnp.float32)


def kernel(
    tok,
    router,
    ids,
    gate,
    up,
    down,
    out,
    z_out,
    wide,
    send1,
    mid1,
    got1,
    rows,
    hidden,
    send2,
    mid2,
    got2,
    weights,
    zs1,
    zs2,
    zs3,
    zg1,
    zg2,
    zg3,
    load_sem,
    p_send,
    p_recv,
    zp_send,
    zp_recv,
    x_send,
    x_recv,
    d_send,
    d_recv,
):
    d = lax.axis_index("dp")
    e = lax.axis_index("expert")
    x, c = d // 2, lax.rem(d, 2)
    z, y = e // RING, lax.rem(e, RING)
    p = y * (1 - c) + z * c
    q = z * (1 - c) + y * c

    def on_p(v):
        return {"dp": d, "expert": (z * RING + v) * (1 - c) + (v * RING + y) * c}

    def on_q(v):
        return {"dp": d, "expert": (v * RING + y) * (1 - c) + (z * RING + v) * c}

    def at_dp(v):
        return {"dp": v, "expert": e}

    def shard(x_at, c_at):
        return 2 * lax.rem(x_at, 4) + c_at

    own, left, right, far = (shard(x + k, c) for k in (0, 3, 1, 2))

    barrier = pltpu.get_barrier_semaphore()
    for k in range(1, RING):
        pl.semaphore_signal(barrier, 1, device_id=on_p(lax.rem(p + k, RING)), device_id_type=MESH)
        pl.semaphore_signal(barrier, 1, device_id=on_q(lax.rem(q + k, RING)), device_id_type=MESH)
        pl.semaphore_signal(barrier, 1, device_id=at_dp(lax.rem(d + k, 8)), device_id_type=MESH)

    def piece(m, dev, first, count):
        start = pl.multiple_of(96 * dev + first, 16)
        return weights.at[m, pl.ds(start, count), :]

    loads = []
    for m, ref in enumerate((gate, up, down)):
        loads.append(pltpu.make_async_copy(ref.at[0], piece(m, own, 0, 96), load_sem.at[m]))
        loads[-1].start()

    logits = dot(tok[...], router[...], NN)
    top = jnp.max(logits, axis=1, keepdims=True)
    log_total = top + jnp.log(jnp.sum(jnp.exp(logits - top), axis=1, keepdims=True))
    local_sum = jnp.sum(log_total * log_total, axis=0, keepdims=True)
    zs1[...] = jnp.broadcast_to(local_sum, zs1.shape)
    zg1[p] = jnp.broadcast_to(local_sum, zs1.shape)
    tokens_here, experts = logits.shape
    lane = lax.broadcasted_iota(jnp.int32, (tokens_here, experts), 1)
    id0, id1 = ids[:, 0:1], ids[:, 1:2]
    hot0, hot1 = id0 == lane, id1 == lane
    chosen0 = jnp.sum(jnp.where(hot0, logits, 0.0), axis=1, keepdims=True)
    chosen1 = jnp.sum(jnp.where(hot1, logits, 0.0), axis=1, keepdims=True)
    peak = jnp.maximum(chosen0, chosen1)
    exp0, exp1 = jnp.exp(chosen0 - peak), jnp.exp(chosen1 - peak)
    weight0, weight1 = exp0 / (exp0 + exp1), exp1 / (exp0 + exp1)

    row_at = lax.broadcasted_iota(jnp.int32, (tokens_here, tokens_here), 0)
    col_at = lax.broadcasted_iota(jnp.int32, (tokens_here, tokens_here), 1)
    earlier = jnp.where(col_at < row_at, 1.0, 0.0).astype(jnp.bfloat16)
    one0 = jnp.where(hot0, 1.0, 0.0)
    one1 = jnp.where(hot1, 1.0, 0.0)
    before0 = dot(earlier, one0.astype(jnp.bfloat16), NN)
    before1 = dot(earlier, one1.astype(jnp.bfloat16), NN) + jnp.sum(one0, axis=0, keepdims=True)
    place0 = jnp.sum(before0 * one0, axis=1, keepdims=True).astype(jnp.int32)
    place1 = jnp.sum(before1 * one1, axis=1, keepdims=True).astype(jnp.int32)

    def ordinal(v):
        return jnp.where(c == 0, (v & 7) * RING + (v >> 3), v)

    slot0 = ordinal(id0) * CAPACITY + place0
    slot1 = ordinal(id1) * CAPACITY + place1
    slot_lane = lax.broadcasted_iota(jnp.int32, (tokens_here, SLOTS), 1)
    in0, in1 = slot0 == slot_lane, slot1 == slot_lane
    picks = jnp.where(in0 | in1, 1.0, 0.0).astype(jnp.bfloat16)
    mix = jnp.where(in0, weight0, jnp.where(in1, weight1, 0.0))
    mix_high = mix.astype(jnp.bfloat16)
    mix_low = (mix - mix_high.astype(jnp.float32)).astype(jnp.bfloat16)

    for n in range(8):
        chunk = dot(picks, tok[:, n * 256 : (n + 1) * 256], TN)
        wide[pl.ds(2 * n, SLOTS, stride=SEGS), :] = chunk[:, :LANES]
        wide[pl.ds(2 * n + 1, SLOTS, stride=SEGS), :] = chunk[:, LANES:]

    def narrow(dst):
        @pl.loop(0, RING)
        def _(a):
            for b in range(RING):
                start = pl.multiple_of((a * RING + b) * BLOCK, BLOCK)
                dst[a, b] = wide[pl.ds(start, BLOCK), :].astype(jnp.bfloat16)

    def to_rows(src):
        @pl.loop(0, RING)
        def _(a):
            for b in range(RING):
                start = pl.multiple_of((a * RING + b) * BLOCK, BLOCK)
                wide[pl.ds(start, BLOCK), :] = src[a, b].astype(jnp.float32)

        for j in range(SEGS):
            part = wide[pl.ds(j, SLOTS, stride=SEGS), :]
            rows[:, j * LANES : (j + 1) * LANES] = part.astype(jnp.bfloat16)

    narrow(send1)
    pl.semaphore_wait(barrier, 3 * (RING - 1))

    def step(phase, src, dst, me, peer):
        copies = []
        for k in OFFSETS:
            v = lax.rem(me + k, RING)
            copies.append(
                pltpu.make_async_remote_copy(
                    src.at[v],
                    dst(me),
                    p_send.at[phase, k],
                    p_recv.at[phase, k],
                    device_id=peer(v),
                    device_id_type=MESH,
                )
            )
            copies[-1].start()
        return copies

    def z_step(phase, src, dst, me, peer):
        copies = []
        for k in range(1, RING):
            v = lax.rem(me + k, RING)
            copies.append(
                pltpu.make_async_remote_copy(
                    src,
                    dst.at[me],
                    zp_send.at[phase, k],
                    zp_recv.at[phase, k],
                    device_id=peer(v),
                    device_id_type=MESH,
                )
            )
            copies[-1].start()
        return copies

    def finish(copies):
        for copy in copies:
            copy.wait()

    def along(m, go_right, stage):
        if go_right:
            dev, first = (own, 0) if stage == 0 else (own, 48) if stage == 1 else (left, 0)
        else:
            dev, first = (own, 48) if stage == 0 else (own, 0) if stage == 1 else (right, 48)
        side = 0 if go_right else 1
        return pltpu.make_async_remote_copy(
            piece(m, dev, first, 48),
            piece(m, dev, first, 48),
            x_send.at[side, m, stage],
            x_recv.at[side, m, stage],
            device_id=at_dp(right if go_right else left),
            device_id_type=MESH,
        )

    def across(m, which):
        dev = (own, left, right, far)[which]
        return pltpu.make_async_remote_copy(
            piece(m, dev, 0, 96),
            piece(m, dev, 0, 96),
            d_send.at[m, which],
            d_recv.at[m, which],
            device_id=at_dp(x * 2 + 1 - c),
            device_id_type=MESH,
        )

    sent = []

    def go(copy):
        copy.start()
        sent.append(copy)

    def own_along(m):
        for stage in (0, 1):
            go(along(m, True, stage))
            go(along(m, False, stage))

    def relay(m):
        along(m, True, 0).wait_recv()
        go(along(m, True, 2))
        along(m, False, 0).wait_recv()
        go(along(m, False, 2))

    def pass_neighbours(m):
        along(m, True, 1).wait_recv()
        go(across(m, 1))
        along(m, False, 1).wait_recv()
        go(across(m, 2))

    def pass_far(m):
        along(m, True, 2).wait_recv()
        along(m, False, 2).wait_recv()
        go(across(m, 3))

    def arrived(m):
        for which in range(4):
            across(m, which).wait_recv()

    for load in loads:
        load.wait()
    own_along(0)
    own_along(1)
    first = step(0, send1, lambda me: mid1.at[:, me], p, on_p)
    z_first = z_step(0, zs1, zg1, p, on_p)
    for m in range(3):
        go(across(m, 0))
    mid1[:, p] = send1[p]
    finish(first)
    finish(z_first)
    z_row = jnp.sum(zg1[...], axis=0)
    zs2[...] = z_row
    zg2[q] = z_row
    second = step(1, mid1, lambda me: got1.at[me], q, on_q)
    relay(0)
    relay(1)
    own_along(2)
    pass_neighbours(0)
    pass_neighbours(1)
    z_second = z_step(1, zs2, zg2, q, on_q)
    got1[q] = mid1[q]
    finish(second)
    finish(z_second)
    z_plane = jnp.sum(zg2[...], axis=0)
    zs3[...] = z_plane
    zg3[d] = z_plane
    relay(2)
    pass_neighbours(2)
    to_rows(got1)
    z_third = z_step(2, zs3, zg3, d, at_dp)
    pass_far(0)
    pass_far(1)
    arrived(0)
    arrived(1)
    for n in range(3):
        cut = slice(n * 256, (n + 1) * 256)
        gated = dot(rows[...], weights[0, cut, :], NT)
        upped = dot(rows[...], weights[1, cut, :], NT)
        hidden[:, cut] = (gated / (1.0 + jnp.exp(-gated)) * upped).astype(jnp.bfloat16)
    pass_far(2)
    arrived(2)
    for n in range(8):
        chunk = dot(hidden[...], weights[2, :, n * 256 : (n + 1) * 256], NN)
        wide[pl.ds(2 * n, SLOTS, stride=SEGS), :] = chunk[:, :LANES]
        wide[pl.ds(2 * n + 1, SLOTS, stride=SEGS), :] = chunk[:, LANES:]
    narrow(send2)
    finish(z_third)
    total = jnp.sum(zg3[...], axis=0)
    z_out[...] = total[0:1, 0:1] / jnp.float32(tokens_here * 512)
    third = step(2, send2, lambda me: mid2.at[:, me], q, on_q)
    mid2[:, q] = send2[q]
    finish(third)
    fourth = step(3, mid2, lambda me: got2.at[me], p, on_p)
    got2[p] = mid2[p]
    for copy in sent:
        copy.wait_send()
    finish(fourth)
    to_rows(got2)
    for n in range(8):
        cut = slice(n * 256, (n + 1) * 256)
        part = rows[:, cut]
        out[:, cut] = (dot(mix_high, part, NN) + dot(mix_low, part, NN)).astype(jnp.bfloat16)


def on_device(tokens, router_weight, route_ids, gate_weight, up_weight, down_weight):
    rows_here, width = tokens.shape
    blocks = (RING, RING, BLOCK, LANES)
    bf16, f32 = jnp.bfloat16, jnp.float32
    vmem = pl.BlockSpec(memory_space=pltpu.VMEM)
    hbm = pl.BlockSpec(memory_space=pl.ANY)
    small = (8, LANES)
    dma = pltpu.SemaphoreType.DMA
    mixture, z_loss = pl.pallas_call(
        kernel,
        out_shape=(
            jax.ShapeDtypeStruct((rows_here, width), bf16),
            jax.ShapeDtypeStruct((1, 1), f32),
        ),
        in_specs=[vmem, vmem, vmem, hbm, hbm, hbm],
        out_specs=(vmem, vmem),
        scratch_shapes=[
            pltpu.VMEM((SLOTS * SEGS, LANES), f32),
            pltpu.VMEM(blocks, bf16),
            pltpu.VMEM(blocks, bf16),
            pltpu.VMEM(blocks, bf16),
            pltpu.VMEM((SLOTS, width), bf16),
            pltpu.VMEM((SLOTS, 768), bf16),
            pltpu.VMEM(blocks, bf16),
            pltpu.VMEM(blocks, bf16),
            pltpu.VMEM(blocks, bf16),
            pltpu.VMEM((3, 768, width), bf16),
            pltpu.VMEM(small, f32),
            pltpu.VMEM(small, f32),
            pltpu.VMEM(small, f32),
            pltpu.VMEM((8,) + small, f32),
            pltpu.VMEM((8,) + small, f32),
            pltpu.VMEM((8,) + small, f32),
            dma((3,)),
            dma((4, RING)),
            dma((4, RING)),
            dma((3, RING)),
            dma((3, RING)),
            dma((2, 3, 3)),
            dma((2, 3, 3)),
            dma((3, 4)),
            dma((3, 4)),
        ],
        compiler_params=pltpu.CompilerParams(
            collective_id=0, has_side_effects=True, vmem_limit_bytes=60 * 1024 * 1024
        ),
    )(tokens, router_weight, route_ids, gate_weight, up_weight, down_weight)
    return mixture, z_loss.reshape(())


def solution(mesh):
    return jax.shard_map(
        on_device,
        mesh=mesh,
        in_specs=(
            P(BOTH, None),
            P(),
            P(BOTH, None),
            P("expert", "dp", None),
            P("expert", "dp", None),
            P("expert", "dp", None),
        ),
        out_specs=(P(BOTH, None), P()),
        check_vma=False,
    )
```

time: 208 us -> 109 us (0.52)
  the two profiles are of different devices: /device:TPU:2 before, /device:TPU:128 now
where the time goes in v1:
time: 109 us
  Pallas kernels  101 us (93%)
  local copies, waits for them, and re-layouts  5.26 us (5%)
  between operations  2.44 us (2%)
    pallas_call x1, Pallas kernels, on_device(): pl.pallas_call(kernel, out_shape=(jax.ShapeDtypeStruct((rows_here, width)...  101 us
    unnamed x3, local copies, waits for them, and re-layouts  5.26 us

profile of v1, /device:TPU:128, one launch (start us, length us, event | category | flops | bytes accessed | tf_op | source)
XLA Modules:
  0.0 109.1 jit_solution(2138142459659071514)
XLA Ops:
  0.6 1.4 %copy.9.ids = s32[128,2]{1,0:T(8,128)} copy(s32[128,2]{0,1:T(2,128)} %param.8) | data formatting | bytes 2048 | tf_op args[2]
  2.1 2.0 %copy.8.router = bf16[2048,64]{1,0:T(8,128)(2,1)} copy(bf16[2048,64]{0,1:T(8,128)(2,1)} %param.7) | data formatting | bytes 524288 | tf_op args[1]
  4.0 101.4 %shard_map.77 = (bf16[128,2048]{1,0:T(8,128)(2,1)}, f32[1,1]{1,0:T(1,128)}) custom-call(bf16[128,2048]{1,0:T(8,128)(2,1)} %tok.1, bf16[2048,64]{1,0:T(8,128)(2,1)} %copy.8.router, s32[128,2]{1,0:T(8,128)} %copy.9.ids, bf16[1,96,2048]{2,1,0:T(8,128)(2,1)} %gate.1, bf16[1,96,2048]{2,1,0:T(8,128)(2,1)} %up.1, bf16[1,96,2048]{2,1,0:T(8,128)(2,1)} %down.1), custom_call_target="tpu_custom_call" | custom-call | tf_op jit(solution)/shard_map/pallas_call | solution.py:332
  105.5 1.9 %copy.12 = bf16[128,2048]{1,0:T(8,128)(2,1)} copy(bf16[128,2048]{1,0:T(8,128)(2,1)} %get-tuple-element.8) | data formatting | bytes 1048576

commit v2 on v1

v2 whole, which is shorter than its diff:
```python
import jax
import jax.numpy as jnp
from jax import lax
from jax.experimental import pallas as pl
from jax.experimental.pallas import tpu as pltpu
from jax.sharding import PartitionSpec as P

MESH = pl.DeviceIdType.MESH
BOTH = ("dp", "expert")
RING = 8
CAPACITY = 5
HALVES = 2
SEGS = 8
LANES = 128
HALF = SEGS * LANES
BLOCK = CAPACITY * SEGS
SLOTS = RING * RING * CAPACITY
FF = 768
NT = (((1,), (1,)), ((), ()))
NN = (((1,), (0,)), ((), ()))
OFFSETS = (4, 3, 5, 2, 6, 1, 7)
scope = jax.named_scope


def dot(a, b, dims):
    return lax.dot_general(a, b, dims, preferred_element_type=jnp.float32)


def kernel(
    tok_hbm,
    router_hbm,
    ids_hbm,
    gate,
    up,
    down,
    out,
    z_out,
    tok,
    router,
    ids,
    wide,
    send1,
    mid1,
    got1,
    rows,
    acc,
    hidden,
    send2,
    mid2,
    got2,
    gate_up,
    downs,
    mixture,
    mix_high,
    mix_low,
    zs1,
    zs2,
    zs3,
    zg1,
    zg2,
    zg3,
    load_sem,
    e_send,
    e_recv,
    z_send,
    z_recv,
    x_send,
    x_recv,
    d_send,
    d_recv,
):
    d = lax.axis_index("dp")
    e = lax.axis_index("expert")
    x, c = d // 2, lax.rem(d, 2)
    z, y = e // RING, lax.rem(e, RING)
    p = y * (1 - c) + z * c
    q = z * (1 - c) + y * c

    def on_p(v):
        return {"dp": d, "expert": (z * RING + v) * (1 - c) + (v * RING + y) * c}

    def on_q(v):
        return {"dp": d, "expert": (v * RING + y) * (1 - c) + (z * RING + v) * c}

    def at_dp(v):
        return {"dp": v, "expert": e}

    def shard(x_at, c_at):
        return 2 * lax.rem(x_at, 4) + c_at

    own, left, right, far = (shard(x + k, c) for k in (0, 3, 1, 2))

    barrier = pltpu.get_barrier_semaphore()
    for k in range(1, RING):
        pl.semaphore_signal(barrier, 1, device_id=on_p(lax.rem(p + k, RING)), device_id_type=MESH)
        pl.semaphore_signal(barrier, 1, device_id=on_q(lax.rem(q + k, RING)), device_id_type=MESH)
        pl.semaphore_signal(barrier, 1, device_id=at_dp(lax.rem(d + k, 8)), device_id_type=MESH)

    inputs = []
    for m, (src, dst) in enumerate(((tok_hbm, tok), (router_hbm, router), (ids_hbm, ids))):
        inputs.append(pltpu.make_async_copy(src, dst, load_sem.at[4 + m]))
        inputs[-1].start()

    def piece(m, dev, first, count):
        part = pl.ds(pl.multiple_of(96 * dev + first, 16), count)
        return gate_up.at[m, part, :] if m < 2 else downs.at[m - 2, part, :]

    loads = []
    for m in range(4):
        src = (gate.at[0], up.at[0], down.at[0, :, 0:HALF], down.at[0, :, HALF:])[m]
        loads.append(pltpu.make_async_copy(src, piece(m, own, 0, 96), load_sem.at[m]))
        loads[-1].start()

    inputs[2].wait()
    experts, tokens_here = router.shape[0], tok.shape[0]
    expert_at = lax.broadcasted_iota(jnp.int32, (experts, tokens_here), 0)
    id0, id1 = ids[0:1, :], ids[1:2, :]
    hot0, hot1 = id0 == expert_at, id1 == expert_at

    row_at = lax.broadcasted_iota(jnp.int32, (tokens_here, tokens_here), 0)
    col_at = lax.broadcasted_iota(jnp.int32, (tokens_here, tokens_here), 1)
    earlier = jnp.where(row_at < col_at, 1.0, 0.0).astype(jnp.bfloat16)
    one0 = jnp.where(hot0, 1.0, 0.0)
    one1 = jnp.where(hot1, 1.0, 0.0)
    before0 = dot(one0.astype(jnp.bfloat16), earlier, NN)
    before1 = dot(one1.astype(jnp.bfloat16), earlier, NN) + jnp.sum(one0, axis=1, keepdims=True)
    place0 = jnp.sum(before0 * one0, axis=0, keepdims=True).astype(jnp.int32)
    place1 = jnp.sum(before1 * one1, axis=0, keepdims=True).astype(jnp.int32)

    def ordinal(v):
        return jnp.where(c == 0, (v & 7) * RING + (v >> 3), v)

    slot0 = ordinal(id0) * CAPACITY + place0
    slot1 = ordinal(id1) * CAPACITY + place1
    slot_at = lax.broadcasted_iota(jnp.int32, (SLOTS, tokens_here), 0)
    in0, in1 = slot0 == slot_at, slot1 == slot_at
    picks = jnp.where(in0 | in1, 1.0, 0.0).astype(jnp.bfloat16)

    def narrow(dst):
        @pl.loop(0, RING)
        def _(a):
            for b in range(RING):
                start = pl.multiple_of((a * RING + b) * BLOCK, BLOCK)
                dst[a, b] = wide[pl.ds(start, BLOCK), :].astype(jnp.bfloat16)

    def spread(n, chunk):
        for i in range(2):
            wide[pl.ds(2 * n + i, SLOTS, stride=SEGS), :] = chunk[:, i * LANES : (i + 1) * LANES]

    def to_rows(src, h):
        @pl.loop(0, RING)
        def _(a):
            for b in range(RING):
                start = pl.multiple_of((a * RING + b) * BLOCK, BLOCK)
                wide[pl.ds(start, BLOCK), :] = src[h, a, b].astype(jnp.float32)

        for j in range(SEGS):
            part = wide[pl.ds(j, SLOTS, stride=SEGS), :]
            cut = slice(h * HALF + j * LANES, h * HALF + (j + 1) * LANES)
            rows[:, cut] = part.astype(jnp.bfloat16)

    def exchange(phase, h, src, dst, me, peer):
        for k in OFFSETS:
            v = lax.rem(me + k, RING)
            pltpu.make_async_remote_copy(
                src.at[h, v],
                dst,
                e_send.at[phase, h],
                e_recv.at[phase, h],
                device_id=peer(v),
                device_id_type=MESH,
            ).start()

    def wait_for(ref, sem):
        pltpu.make_async_copy(ref, ref, sem).wait()

    def landed(phase, h):
        wait_for(send1.at[h, pl.ds(0, RING - 1)], e_recv.at[phase, h])

    def out_of(phase, h):
        wait_for(send1.at[h, pl.ds(0, RING - 1)], e_send.at[phase, h])

    def z_exchange(phase, src, dst, me, peer):
        for k in range(1, RING):
            v = lax.rem(me + k, RING)
            pltpu.make_async_remote_copy(
                src,
                dst.at[me],
                z_send.at[phase],
                z_recv.at[phase],
                device_id=peer(v),
                device_id_type=MESH,
            ).start()

    def z_landed(phase):
        wait_for(zg1.at[pl.ds(0, RING - 1)], z_recv.at[phase])

    def along(m, go_right, stage):
        if go_right:
            dev, first = (own, 0) if stage == 0 else (own, 48) if stage == 1 else (left, 0)
        else:
            dev, first = (own, 48) if stage == 0 else (own, 0) if stage == 1 else (right, 48)
        side = 0 if go_right else 1
        return pltpu.make_async_remote_copy(
            piece(m, dev, first, 48),
            piece(m, dev, first, 48),
            x_send.at[m],
            x_recv.at[side, m, stage],
            device_id=at_dp(right if go_right else left),
            device_id_type=MESH,
        )

    def across(m, which):
        dev = (own, left, right, far)[which]
        return pltpu.make_async_remote_copy(
            piece(m, dev, 0, 96),
            piece(m, dev, 0, 96),
            d_send.at[m],
            d_recv.at[m],
            device_id=at_dp(x * 2 + 1 - c),
            device_id_type=MESH,
        )

    def go(copy):
        copy.start()

    def own_along(m, stage):
        go(along(m, True, stage))
        go(along(m, False, stage))

    def relay(m):
        along(m, True, 0).wait_recv()
        go(along(m, True, 2))
        along(m, False, 0).wait_recv()
        go(along(m, False, 2))

    def pass_neighbours(m):
        along(m, True, 1).wait_recv()
        go(across(m, 1))
        along(m, False, 1).wait_recv()
        go(across(m, 2))

    def pass_far(m):
        along(m, True, 2).wait_recv()
        along(m, False, 2).wait_recv()
        go(across(m, 3))

    def rows_of(m, count):
        return gate_up.at[m, pl.ds(0, count)] if m < 2 else downs.at[m - 2, pl.ds(0, count)]

    def arrived(m):
        wait_for(rows_of(m, 4 * 96), d_recv.at[m])

    def dispatch(h):
        for n in range(SEGS // 2):
            cut = slice(h * HALF + n * 256, h * HALF + (n + 1) * 256)
            spread(n, dot(picks, tok[:, cut], NN))
        narrow(send1.at[h])

    inputs[0].wait()
    with scope("dispatch0"):
        dispatch(0)
    with scope("barrier"):
        pl.semaphore_wait(barrier, 3 * (RING - 1))
    for load in loads:
        load.wait()
    for m in range(2):
        own_along(m, 0)
        own_along(m, 1)
    exchange(0, 0, send1, mid1.at[0, :, p], p, on_p)
    with scope("dispatch1"):
        dispatch(1)
    inputs[1].wait()
    exchange(0, 1, send1, mid1.at[1, :, p], p, on_p)
    for m in range(4):
        go(across(m, 0))
    with scope("router"):
        for h in range(HALVES):
            mid1[h, :, p] = send1[h, p]
        logits = dot(router[...], tok[...], NT)
        top = jnp.max(logits, axis=0, keepdims=True)
        log_total = top + jnp.log(jnp.sum(jnp.exp(logits - top), axis=0, keepdims=True))
        local_sum = jnp.sum(log_total * log_total, axis=1, keepdims=True)
        zs1[...] = jnp.broadcast_to(local_sum, zs1.shape)
        zg1[p] = jnp.broadcast_to(local_sum, zs1.shape)
        chosen0 = jnp.sum(jnp.where(hot0, logits, 0.0), axis=0, keepdims=True)
        chosen1 = jnp.sum(jnp.where(hot1, logits, 0.0), axis=0, keepdims=True)
        peak = jnp.maximum(chosen0, chosen1)
        exp0, exp1 = jnp.exp(chosen0 - peak), jnp.exp(chosen1 - peak)
        weight0, weight1 = exp0 / (exp0 + exp1), exp1 / (exp0 + exp1)
        mix = jnp.where(in0, weight0, jnp.where(in1, weight1, 0.0)).T
        mix_high[...] = mix.astype(jnp.bfloat16)
        mix_low[...] = (mix - mix.astype(jnp.bfloat16).astype(jnp.float32)).astype(jnp.bfloat16)
    with scope("relay_g"):
        relay(0)
    z_exchange(0, zs1, zg1, p, on_p)
    with scope("p1_0"):
        landed(0, 0)
    with scope("p1_1s"):
        out_of(0, 1)
    exchange(1, 0, mid1, got1.at[0, q], q, on_q)
    with scope("relay_u"):
        relay(1)
        pass_neighbours(0)
    with scope("p1_1"):
        landed(0, 1)
    exchange(1, 1, mid1, got1.at[1, q], q, on_q)
    own_along(2, 0)
    own_along(2, 1)
    for h in range(HALVES):
        got1[h, q] = mid1[h, q]
    with scope("pass_u"):
        pass_neighbours(1)
    with scope("far_g"):
        pass_far(0)
    z_landed(0)
    z_row = jnp.sum(zg1[...], axis=0)
    zs2[...] = z_row
    zg2[q] = z_row
    with scope("p2_0"):
        landed(1, 0)
    with scope("rows_0"):
        to_rows(got1, 0)
    z_exchange(1, zs2, zg2, q, on_q)
    with scope("far_u"):
        pass_far(1)
    with scope("relay_d0"):
        relay(2)
    own_along(3, 0)
    own_along(3, 1)

    def project(h, m, n):
        across_k = slice(h * HALF, (h + 1) * HALF)
        return dot(rows[:, across_k], gate_up[m, n * 256 : (n + 1) * 256, across_k], NT)

    for m in range(2):
        with scope("arrived_%d" % m):
            arrived(m)
        with scope("ffn_0%d" % m):
            for n in range(FF // 256):
                acc[m, :, n * 256 : (n + 1) * 256] = project(0, m, n)
    with scope("pass_d0"):
        pass_neighbours(2)
    with scope("p2_1"):
        landed(1, 1)
    with scope("rows_1"):
        to_rows(got1, 1)
    with scope("far_d0"):
        pass_far(2)
    with scope("ffn_1"):
        for n in range(FF // 256):
            cut = slice(n * 256, (n + 1) * 256)
            gated = acc[0, :, cut] + project(1, 0, n)
            upped = acc[1, :, cut] + project(1, 1, n)
            hidden[:, cut] = (gated / (1.0 + jnp.exp(-gated)) * upped).astype(jnp.bfloat16)
    for h in range(HALVES):
        with scope("far_d%d" % h):
            if h == 1:
                relay(3)
                pass_neighbours(3)
                pass_far(3)
        with scope("arrived_d%d" % h):
            arrived(2 + h)
        with scope("down_%d" % h):
            for n in range(SEGS // 2):
                spread(n, dot(hidden[...], downs[h, :, n * 256 : (n + 1) * 256], NN))
            narrow(send2.at[h])
        exchange(2, h, send2, mid2.at[h, :, q], q, on_q)
    z_landed(1)
    z_plane = jnp.sum(zg2[...], axis=0)
    zs3[...] = z_plane
    zg3[d] = z_plane
    for h in range(HALVES):
        mid2[h, :, q] = send2[h, q]
    z_exchange(2, zs3, zg3, d, at_dp)
    with scope("p3_0"):
        landed(2, 0)
    with scope("p3_1s"):
        out_of(2, 1)
    exchange(3, 0, mid2, got2.at[0, p], p, on_p)
    z_landed(2)
    total = jnp.sum(zg3[...], axis=0)
    z_out[...] = total[0:1, 0:1] / jnp.float32(tokens_here * 512)
    with scope("p3_1"):
        landed(2, 1)
    exchange(3, 1, mid2, got2.at[1, p], p, on_p)
    for h in range(HALVES):
        got2[h, p] = mid2[h, p]
    with scope("outs"):
        out_of(0, 0)
        out_of(1, 0)
        out_of(1, 1)
        out_of(2, 0)
        for phase in range(3):
            wait_for(zg1.at[pl.ds(0, RING - 1)], z_send.at[phase])
        for m in range(4):
            wait_for(rows_of(m, 6 * 48), x_send.at[m])
            wait_for(rows_of(m, 4 * 96), d_send.at[m])
    stores = []
    for h in range(HALVES):
        with scope("p4_%d" % h):
            landed(3, h)
        with scope("rows2_%d" % h):
            to_rows(got2, h)
        with scope("mix_%d" % h):
            for n in range(SEGS // 2):
                cut = slice(h * HALF + n * 256, h * HALF + (n + 1) * 256)
                part = rows[:, cut]
                mixed = dot(mix_high[...], part, NN) + dot(mix_low[...], part, NN)
                mixture[:, cut] = mixed.astype(jnp.bfloat16)
        cut = slice(h * HALF, (h + 1) * HALF)
        stores.append(pltpu.make_async_copy(mixture.at[:, cut], out.at[:, cut], load_sem.at[h]))
        stores[-1].start()
    with scope("end"):
        out_of(3, 0)
        out_of(3, 1)
        for store in stores:
            store.wait()


def on_device(tokens, router_weight, route_ids, gate_weight, up_weight, down_weight):
    rows_here, width = tokens.shape
    blocks = (HALVES, RING, RING, BLOCK, LANES)
    bf16, f32 = jnp.bfloat16, jnp.float32
    vmem = pl.BlockSpec(memory_space=pltpu.VMEM)
    hbm = pl.BlockSpec(memory_space=pltpu.HBM)
    small = (8, LANES)
    dma = pltpu.SemaphoreType.DMA
    mixture, z_loss = pl.pallas_call(
        kernel,
        out_shape=(
            jax.ShapeDtypeStruct((rows_here, width), bf16),
            jax.ShapeDtypeStruct((1, 1), f32),
        ),
        in_specs=[hbm] * 6,
        out_specs=(hbm, vmem),
        scratch_shapes=[
            pltpu.VMEM((rows_here, width), bf16),
            pltpu.VMEM(router_weight.shape[::-1], bf16),
            pltpu.VMEM(route_ids.shape[::-1], jnp.int32),
            pltpu.VMEM((SLOTS * SEGS, LANES), f32),
            pltpu.VMEM(blocks, bf16),
            pltpu.VMEM(blocks, bf16),
            pltpu.VMEM(blocks, bf16),
            pltpu.VMEM((SLOTS, width), bf16),
            pltpu.VMEM((2, SLOTS, FF), f32),
            pltpu.VMEM((SLOTS, FF), bf16),
            pltpu.VMEM(blocks, bf16),
            pltpu.VMEM(blocks, bf16),
            pltpu.VMEM(blocks, bf16),
            pltpu.VMEM((2, FF, width), bf16),
            pltpu.VMEM((HALVES, FF, HALF), bf16),
            pltpu.VMEM((rows_here, width), bf16),
            pltpu.VMEM((rows_here, SLOTS), bf16),
            pltpu.VMEM((rows_here, SLOTS), bf16),
            pltpu.VMEM(small, f32),
            pltpu.VMEM(small, f32),
            pltpu.VMEM(small, f32),
            pltpu.VMEM((8,) + small, f32),
            pltpu.VMEM((8,) + small, f32),
            pltpu.VMEM((8,) + small, f32),
            dma((7,)),
            dma((4, HALVES)),
            dma((4, HALVES)),
            dma((3,)),
            dma((3,)),
            dma((4,)),
            dma((2, 4, 3)),
            dma((4,)),
            dma((4,)),
        ],
        compiler_params=pltpu.CompilerParams(
            collective_id=0, has_side_effects=True, vmem_limit_bytes=60 * 1024 * 1024
        ),
    )(tokens, router_weight.T, route_ids.T, gate_weight, up_weight, down_weight)
    return mixture, z_loss.reshape(())


def solution(mesh):
    return jax.shard_map(
        on_device,
        mesh=mesh,
        in_specs=(
            P(BOTH, None),
            P(),
            P(BOTH, None),
            P("expert", "dp", None),
            P("expert", "dp", None),
            P("expert", "dp", None),
        ),
        out_specs=(P(BOTH, None), P()),
        check_vma=False,
    )
```

time: 109 us -> 91.9 us (0.84)
  the two profiles are of different devices: /device:TPU:128 before, /device:TPU:1 now
where the time goes in v2:
time: 91.9 us; the launch traced here: 91.7 us
  Pallas kernels  87.5 us (95%)
  between operations  2.34 us (3%)
  local copies, waits for them, and re-layouts  1.88 us (2%)
    pallas_call x1, Pallas kernels, on_device(): pl.pallas_call(kernel, out_shape=(jax.ShapeDtypeStruct((rows_here, width)...  87.5 us
    unnamed x1, local copies, waits for them, and re-layouts  1.88 us

profile of v2, /device:TPU:1, one launch (start us, length us, event | category | flops | bytes accessed | tf_op | source)
XLA Modules:
  0.0 91.7 jit_solution(10039409872285431500)
XLA Ops:
  0.6 87.5 %shard_map.77 = (bf16[128,2048]{1,0:T(8,128)(2,1)}, f32[1,1]{1,0:T(1,128)}) custom-call(bf16[128,2048]{1,0:T(8,128)(2,1)} %tok_hbm.1, bf16[64,2048]{1,0:T(8,128)(2,1)} %bitcast.3, s32[2,128]{1,0:T(2,128)} %bitcast.4, bf16[1,96,2048]{2,1,0:T(8,128)(2,1)} %gate.1, bf16[1,96,2048]{2,1,0:T(8,128)(2,1)} %up.1, bf16[1,96,2048]{2,1,0:T(8,128)(2,1)} %down.1), custom_call_target="tpu_custom_call" | custom-call | tf_op jit(solution)/shard_map/pallas_call | solution.py:429
  88.1 1.9 %copy.10 = bf16[128,2048]{1,0:T(8,128)(2,1)} copy(bf16[128,2048]{1,0:T(8,128)(2,1)} %get-tuple-element.8) | data formatting | bytes 1048576

commit v3 on v2

--- a/solution.py
+++ b/solution.py
@@ -19,6 +19,7 @@
 NT = (((1,), (1,)), ((), ()))
 NN = (((1,), (0,)), ((), ()))
 OFFSETS = (4, 3, 5, 2, 6, 1, 7)
+EARLY = OFFSETS[:5]
 scope = jax.named_scope
 
 
@@ -53,6 +54,7 @@
     mixture,
     mix_high,
     mix_low,
+    z_val,
     zs1,
     zs2,
     zs3,
@@ -68,6 +70,8 @@
     x_recv,
     d_send,
     d_recv,
+    line,
+    plane,
 ):
     d = lax.axis_index("dp")
     e = lax.axis_index("expert")
@@ -90,16 +94,44 @@
 
     own, left, right, far = (shard(x + k, c) for k in (0, 3, 1, 2))
 
-    barrier = pltpu.get_barrier_semaphore()
-    for k in range(1, RING):
-        pl.semaphore_signal(barrier, 1, device_id=on_p(lax.rem(p + k, RING)), device_id_type=MESH)
-        pl.semaphore_signal(barrier, 1, device_id=on_q(lax.rem(q + k, RING)), device_id_type=MESH)
-        pl.semaphore_signal(barrier, 1, device_id=at_dp(lax.rem(d + k, 8)), device_id_type=MESH)
-
     inputs = []
-    for m, (src, dst) in enumerate(((tok_hbm, tok), (router_hbm, router), (ids_hbm, ids))):
+    for m, (src, dst) in enumerate(((ids_hbm, ids), (tok_hbm, tok), (router_hbm, router))):
         inputs.append(pltpu.make_async_copy(src, dst, load_sem.at[4 + m]))
         inputs[-1].start()
+
+    barrier = pltpu.get_barrier_semaphore()
+    other = at_dp(x * 2 + 1 - c)
+    for k in OFFSETS:
+        for peer in (z * RING + lax.rem(y + k, RING), lax.rem(z + k, RING) * RING + y):
+            pl.semaphore_signal(
+                barrier, 1, device_id={"dp": x * 2 + 1, "expert": peer}, device_id_type=MESH
+            )
+    for k in range(1, 4):
+        pl.semaphore_signal(barrier, 1, device_id=at_dp(shard(x + k, 0)), device_id_type=MESH)
+
+    @pl.when(c == 1)
+    def _():
+        pl.semaphore_signal(barrier, 1, device_id=other, device_id_type=MESH)
+
+    def line_here():
+        @pl.when(c == 0)
+        def _():
+            pl.semaphore_wait(barrier, 7)
+            pl.semaphore_signal(line, 1, device_id=other, device_id_type=MESH)
+
+        @pl.when(c == 1)
+        def _():
+            pl.semaphore_wait(line, 1)
+
+    def plane_here():
+        @pl.when(c == 1)
+        def _():
+            pl.semaphore_wait(barrier, 4 * (RING - 1))
+            pl.semaphore_signal(plane, 1, device_id=other, device_id_type=MESH)
+
+        @pl.when(c == 0)
+        def _():
+            pl.semaphore_wait(plane, 1)
 
     def piece(m, dev, first, count):
         part = pl.ds(pl.multiple_of(96 * dev + first, 16), count)
@@ -111,7 +143,8 @@
         loads.append(pltpu.make_async_copy(src, piece(m, own, 0, 96), load_sem.at[m]))
         loads[-1].start()
 
-    inputs[2].wait()
+    with scope("ids_wait"):
+        inputs[0].wait()
     experts, tokens_here = router.shape[0], tok.shape[0]
     expert_at = lax.broadcasted_iota(jnp.int32, (experts, tokens_here), 0)
     id0, id1 = ids[0:1, :], ids[1:2, :]
@@ -165,7 +198,7 @@
             pltpu.make_async_remote_copy(
                 src.at[h, v],
                 dst,
-                e_send.at[phase, h],
+                e_send.at[phase, h, 0 if k in EARLY else 1],
                 e_recv.at[phase, h],
                 device_id=peer(v),
                 device_id_type=MESH,
@@ -177,8 +210,17 @@
     def landed(phase, h):
         wait_for(send1.at[h, pl.ds(0, RING - 1)], e_recv.at[phase, h])
 
+    def early_out(phase, h):
+        wait_for(send1.at[h, pl.ds(0, len(EARLY))], e_send.at[phase, h, 0])
+
+    def late_out(phase, h):
+        if len(EARLY) == RING - 1:
+            return
+        wait_for(send1.at[h, pl.ds(0, RING - 1 - len(EARLY))], e_send.at[phase, h, 1])
+
     def out_of(phase, h):
-        wait_for(send1.at[h, pl.ds(0, RING - 1)], e_send.at[phase, h])
+        early_out(phase, h)
+        late_out(phase, h)
 
     def z_exchange(phase, src, dst, me, peer):
         for k in range(1, RING):
@@ -257,20 +299,24 @@
             spread(n, dot(picks, tok[:, cut], NN))
         narrow(send1.at[h])
 
-    inputs[0].wait()
+    with scope("line"):
+        line_here()
+    with scope("load_wait"):
+        for load in loads:
+            load.wait()
+    for m in range(3):
+        own_along(m, 0)
+    own_along(0, 1)
+    with scope("tok_wait"):
+        inputs[1].wait()
     with scope("dispatch0"):
         dispatch(0)
-    with scope("barrier"):
-        pl.semaphore_wait(barrier, 3 * (RING - 1))
-    for load in loads:
-        load.wait()
-    for m in range(2):
-        own_along(m, 0)
-        own_along(m, 1)
+    with scope("plane"):
+        plane_here()
     exchange(0, 0, send1, mid1.at[0, :, p], p, on_p)
     with scope("dispatch1"):
         dispatch(1)
-    inputs[1].wait()
+    inputs[2].wait()
     exchange(0, 1, send1, mid1.at[1, :, p], p, on_p)
     for m in range(4):
         go(across(m, 0))
@@ -291,27 +337,28 @@
         mix = jnp.where(in0, weight0, jnp.where(in1, weight1, 0.0)).T
         mix_high[...] = mix.astype(jnp.bfloat16)
         mix_low[...] = (mix - mix.astype(jnp.bfloat16).astype(jnp.float32)).astype(jnp.bfloat16)
-    with scope("relay_g"):
-        relay(0)
     z_exchange(0, zs1, zg1, p, on_p)
     with scope("p1_0"):
         landed(0, 0)
+    with scope("relay_gu"):
+        relay(0)
+        relay(1)
+    own_along(1, 1)
     with scope("p1_1s"):
-        out_of(0, 1)
+        early_out(0, 1)
     exchange(1, 0, mid1, got1.at[0, q], q, on_q)
-    with scope("relay_u"):
-        relay(1)
-        pass_neighbours(0)
+    with scope("relay_d0"):
+        relay(2)
+    own_along(2, 1)
+    own_along(3, 0)
+    own_along(3, 1)
     with scope("p1_1"):
         landed(0, 1)
     exchange(1, 1, mid1, got1.at[1, q], q, on_q)
-    own_along(2, 0)
-    own_along(2, 1)
     for h in range(HALVES):
         got1[h, q] = mid1[h, q]
-    with scope("pass_u"):
-        pass_neighbours(1)
-    with scope("far_g"):
+    with scope("pass_g"):
+        pass_neighbours(0)
         pass_far(0)
     z_landed(0)
     z_row = jnp.sum(zg1[...], axis=0)
@@ -324,29 +371,32 @@
     z_exchange(1, zs2, zg2, q, on_q)
     with scope("far_u"):
         pass_far(1)
-    with scope("relay_d0"):
-        relay(2)
-    own_along(3, 0)
-    own_along(3, 1)
 
     def project(h, m, n):
         across_k = slice(h * HALF, (h + 1) * HALF)
         return dot(rows[:, across_k], gate_up[m, n * 256 : (n + 1) * 256, across_k], NT)
 
-    for m in range(2):
-        with scope("arrived_%d" % m):
-            arrived(m)
+    def first_half(m):
         with scope("ffn_0%d" % m):
             for n in range(FF // 256):
                 acc[m, :, n * 256 : (n + 1) * 256] = project(0, m, n)
+
+    with scope("arrived_0"):
+        arrived(0)
+    first_half(0)
+    with scope("pass_u"):
+        pass_neighbours(1)
+    with scope("arrived_1"):
+        arrived(1)
+    first_half(1)
+    with scope("far_d0"):
+        pass_far(2)
+    with scope("p2_1"):
+        landed(1, 1)
     with scope("pass_d0"):
         pass_neighbours(2)
-    with scope("p2_1"):
-        landed(1, 1)
     with scope("rows_1"):
         to_rows(got1, 1)
-    with scope("far_d0"):
-        pass_far(2)
     with scope("ffn_1"):
         for n in range(FF // 256):
             cut = slice(n * 256, (n + 1) * 256)
@@ -376,11 +426,12 @@
     with scope("p3_0"):
         landed(2, 0)
     with scope("p3_1s"):
-        out_of(2, 1)
+        early_out(2, 1)
     exchange(3, 0, mid2, got2.at[0, p], p, on_p)
     z_landed(2)
     total = jnp.sum(zg3[...], axis=0)
-    z_out[...] = total[0:1, 0:1] / jnp.float32(tokens_here * 512)
+    z_val[...] = total[0:1, :] / jnp.float32(tokens_here * 512)
+    z_store = pltpu.make_async_copy(z_val, z_out, load_sem.at[2])
     with scope("p3_1"):
         landed(2, 1)
     exchange(3, 1, mid2, got2.at[1, p], p, on_p)
@@ -388,6 +439,8 @@
         got2[h, p] = mid2[h, p]
     with scope("outs"):
         out_of(0, 0)
+        late_out(0, 1)
+        late_out(2, 1)
         out_of(1, 0)
         out_of(1, 1)
         out_of(2, 0)
@@ -396,7 +449,8 @@
         for m in range(4):
             wait_for(rows_of(m, 6 * 48), x_send.at[m])
             wait_for(rows_of(m, 4 * 96), d_send.at[m])
-    stores = []
+    z_store.start()
+    stores = [z_store]
     for h in range(HALVES):
         with scope("p4_%d" % h):
             landed(3, h)
@@ -422,7 +476,6 @@
     rows_here, width = tokens.shape
     blocks = (HALVES, RING, RING, BLOCK, LANES)
     bf16, f32 = jnp.bfloat16, jnp.float32
-    vmem = pl.BlockSpec(memory_space=pltpu.VMEM)
     hbm = pl.BlockSpec(memory_space=pltpu.HBM)
     small = (8, LANES)
     dma = pltpu.SemaphoreType.DMA
@@ -430,10 +483,10 @@
         kernel,
         out_shape=(
             jax.ShapeDtypeStruct((rows_here, width), bf16),
-            jax.ShapeDtypeStruct((1, 1), f32),
+            jax.ShapeDtypeStruct((1, LANES), f32),
         ),
         in_specs=[hbm] * 6,
-        out_specs=(hbm, vmem),
+        out_specs=(hbm, hbm),
         scratch_shapes=[
             pltpu.VMEM((rows_here, width), bf16),
             pltpu.VMEM(router_weight.shape[::-1], bf16),
@@ -453,6 +506,7 @@
             pltpu.VMEM((rows_here, width), bf16),
             pltpu.VMEM((rows_here, SLOTS), bf16),
             pltpu.VMEM((rows_here, SLOTS), bf16),
+            pltpu.VMEM((1, LANES), f32),
             pltpu.VMEM(small, f32),
             pltpu.VMEM(small, f32),
             pltpu.VMEM(small, f32),
@@ -460,7 +514,7 @@
             pltpu.VMEM((8,) + small, f32),
             pltpu.VMEM((8,) + small, f32),
             dma((7,)),
-            dma((4, HALVES)),
+            dma((4, HALVES, 2)),
             dma((4, HALVES)),
             dma((3,)),
             dma((3,)),
@@ -468,12 +522,14 @@
             dma((2, 4, 3)),
             dma((4,)),
             dma((4,)),
+            pltpu.SemaphoreType.REGULAR,
+            pltpu.SemaphoreType.REGULAR,
         ],
         compiler_params=pltpu.CompilerParams(
             collective_id=0, has_side_effects=True, vmem_limit_bytes=60 * 1024 * 1024
         ),
     )(tokens, router_weight.T, route_ids.T, gate_weight, up_weight, down_weight)
-    return mixture, z_loss.reshape(())
+    return mixture, z_loss[0, 0]
 
 
 def solution(mesh):

time: 91.9 us -> 87.3 us (0.950)
  Pallas kernels: 87.5 us -> 82.5 us
    pallas_call x1, Pallas kernels: 87.5 us -> 82.5 us  [on_device(): pl.pallas_call(kernel, out_shape=(jax.ShapeDtypeStruct((rows_here, width)...]
    unnamed x1 -> x3, local copies, waits for them, and re-layouts: 1.88 us -> 1.89 us
where the time goes in v3:
time: 87.3 us; the launch traced here: 86.2 us
  Pallas kernels  82.5 us (95%)
  local copies, waits for them, and re-layouts  1.89 us (2%)
  between operations  1.81 us (2%)
    pallas_call x1, Pallas kernels, on_device(): pl.pallas_call(kernel, out_shape=(jax.ShapeDtypeStruct((rows_here, width)...  82.5 us
    unnamed x3, local copies, waits for them, and re-layouts  1.89 us

profile of v3, /device:TPU:1, one launch (start us, length us, event | category | flops | bytes accessed | tf_op | source)
XLA Modules:
  0.0 86.2 jit_solution(6107591090228730476)
XLA Ops:
  0.6 82.5 %shard_map.77 = (bf16[128,2048]{1,0:T(8,128)(2,1)}, f32[1,128]{1,0:T(1,128)}) custom-call(bf16[128,2048]{1,0:T(8,128)(2,1)} %tok_hbm.1, bf16[64,2048]{1,0:T(8,128)(2,1)} %bitcast.4, s32[2,128]{1,0:T(2,128)} %bitcast.5, bf16[1,96,2048]{2,1,0:T(8,128)(2,1)} %gate.1, bf16[1,96,2048]{2,1,0:T(8,128)(2,1)} %up.1, bf16[1,96,2048]{2,1,0:T(8,128)(2,1)} %down.1), custom_call_target="tpu_custom_call" | custom-call | tf_op jit(solution)/shard_map/pallas_call | solution.py:482
  83.2 0.0 copy-start
  83.2 1.9 %copy.10 = bf16[128,2048]{1,0:T(8,128)(2,1)} copy(bf16[128,2048]{1,0:T(8,128)(2,1)} %get-tuple-element.8) | data formatting | bytes 1048576
  85.1 0.0 copy-done
Async XLA Ops:
  83.2 1.9 %copy-start = (f32[1,128]{1,0:T(1,128)S(1)}, f32[1,128]{1,0:T(1,128)}, u32[]{:S(2)}) copy-start(f32[1,128]{1,0:T(1,128)} %get-tuple-element.5) | copy-start | bytes 1540

commit v4 on v3

--- a/solution.py
+++ b/solution.py
@@ -18,7 +18,7 @@
 FF = 768
 NT = (((1,), (1,)), ((), ()))
 NN = (((1,), (0,)), ((), ()))
-OFFSETS = (4, 3, 5, 2, 6, 1, 7)
+OFFSETS = (3, 5, 4, 2, 6, 1, 7)
 EARLY = OFFSETS[:5]
 scope = jax.named_scope
 
@@ -34,7 +34,10 @@
     gate,
     up,
     down,
-    out,
+    out0,
+    out1,
+    out2,
+    out3,
     z_out,
     tok,
     router,
@@ -51,7 +54,6 @@
     got2,
     gate_up,
     downs,
-    mixture,
     mix_high,
     mix_low,
     z_val,
@@ -73,6 +75,7 @@
     line,
     plane,
 ):
+    outs = (out0, out1, out2, out3)
     d = lax.axis_index("dp")
     e = lax.axis_index("expert")
     x, c = d // 2, lax.rem(d, 2)
@@ -461,10 +464,8 @@
                 cut = slice(h * HALF + n * 256, h * HALF + (n + 1) * 256)
                 part = rows[:, cut]
                 mixed = dot(mix_high[...], part, NN) + dot(mix_low[...], part, NN)
-                mixture[:, cut] = mixed.astype(jnp.bfloat16)
-        cut = slice(h * HALF, (h + 1) * HALF)
-        stores.append(pltpu.make_async_copy(mixture.at[:, cut], out.at[:, cut], load_sem.at[h]))
-        stores[-1].start()
+                piece_at, first = divmod(h * HALF + n * 256, 512)
+                outs[piece_at][:, first : first + 256] = mixed.astype(jnp.bfloat16)
     with scope("end"):
         out_of(3, 0)
         out_of(3, 1)
@@ -476,17 +477,18 @@
     rows_here, width = tokens.shape
     blocks = (HALVES, RING, RING, BLOCK, LANES)
     bf16, f32 = jnp.bfloat16, jnp.float32
+    vmem = pl.BlockSpec(memory_space=pltpu.VMEM)
     hbm = pl.BlockSpec(memory_space=pltpu.HBM)
     small = (8, LANES)
     dma = pltpu.SemaphoreType.DMA
-    mixture, z_loss = pl.pallas_call(
+    *pieces, z_loss = pl.pallas_call(
         kernel,
         out_shape=(
-            jax.ShapeDtypeStruct((rows_here, width), bf16),
+            *[jax.ShapeDtypeStruct((rows_here, width // 4), bf16)] * 4,
             jax.ShapeDtypeStruct((1, LANES), f32),
         ),
         in_specs=[hbm] * 6,
-        out_specs=(hbm, hbm),
+        out_specs=(*[vmem] * 4, hbm),
         scratch_shapes=[
             pltpu.VMEM((rows_here, width), bf16),
             pltpu.VMEM(router_weight.shape[::-1], bf16),
@@ -503,7 +505,6 @@
             pltpu.VMEM(blocks, bf16),
             pltpu.VMEM((2, FF, width), bf16),
             pltpu.VMEM((HALVES, FF, HALF), bf16),
-            pltpu.VMEM((rows_here, width), bf16),
             pltpu.VMEM((rows_here, SLOTS), bf16),
             pltpu.VMEM((rows_here, SLOTS), bf16),
             pltpu.VMEM((1, LANES), f32),
@@ -526,10 +527,10 @@
             pltpu.SemaphoreType.REGULAR,
         ],
         compiler_params=pltpu.CompilerParams(
-            collective_id=0, has_side_effects=True, vmem_limit_bytes=60 * 1024 * 1024
+            collective_id=0, has_side_effects=True, vmem_limit_bytes=55889100
         ),
     )(tokens, router_weight.T, route_ids.T, gate_weight, up_weight, down_weight)
-    return mixture, z_loss[0, 0]
+    return jnp.concatenate(pieces, axis=1), z_loss[0, 0]
 
 
 def solution(mesh):

time: 87.3 us -> 85.8 us (0.983); the launches traced: 86.2 us -> 85.6 us
  local copies, waits for them, and re-layouts: 1.89 us -> 0.67 us
    unnamed x3 -> x2, local copies, waits for them, and re-layouts: 1.89 us -> 0.67 us
where the time goes in v4:
time: 85.8 us; the launch traced here: 85.6 us
  Pallas kernels  82.3 us (96%)
  between operations  1.81 us (2%)
    pallas_call x1, Pallas kernels, on_device(): pl.pallas_call(kernel, out_shape=(*[jax.ShapeDtypeStruct((rows_here, widt...  82.3 us

profile of v4, /device:TPU:1, one launch (start us, length us, event | category | flops | bytes accessed | tf_op | source)
XLA Modules:
  0.0 85.6 jit_solution(7712552972983196672)
XLA Ops:
  0.6 0.0 copy-start
  0.6 0.7 copy-done
  1.3 82.3 %shard_map.77 = (bf16[128,512]{1,0:T(8,128)(2,1)S(1)}, bf16[128,512]{1,0:T(8,128)(2,1)S(1)}, bf16[128,512]{1,0:T(8,128)(2,1)S(1)}, bf16[128,512]{1,0:T(8,128)(2,1)S(1)}, f32[1,128]{1,0:T(1,128)S(1)}) custom-call(bf16[128,2048]{1,0:T(8,128)(2,1)} %tok_hbm.1, bf16[64,2048]{1,0:T(8,128)(2,1)} %bitcast.6, s32[2,128]{1,0:T(2,128)S(1)} %bitcast.4, ...), custom_call_target="tpu_custom_call" | custom-call | tf_op jit(solution)/shard_map/pallas_call | solution.py:484
  83.6 0.8 pad_maximum_fusion
Async XLA Ops:
  0.6 0.7 copy-start
